TPU v7x, 256 devices: a whole 4x4x8 slice. The times are simulated.
256 devices in a mesh: dp: 64 (over z, y, core), comp: 4 (over x).
Axes of the slice: x: 4, y: 4, z: 8, core: 2. Of those that a mesh axis runs over, the one named last changes fastest.
Arguments:
- points: float32 [65536, 128], P('dp'), may hold values from -64 to 64
- block_counts: int32 [64], replicated, may hold values from 1 to 16, as said below
- block_dest: int32 [64, 16], replicated, may hold values from 0 to 63, as said below
- means: float32 [256, 128], P(('dp', 'comp')), may hold values from -3 to 3
- factors: float32 [256, 128, 128], P(('dp', 'comp')), may hold values from -0.25 to 1.4, as said below
- log_weights: float32 [256], P(('dp', 'comp')), may hold values from -4 to 4
Outputs:
- new_means: float32 [256, 128], P(('dp', 'comp'))
- new_factors: float32 [256, 128, 128], P(('dp', 'comp'))
- new_log_weights: float32 [256], P(('dp', 'comp'))
- log_density: float32 [16384], P('dp')
Inputs may be any that keep to these rules, and one draw needn't show every extreme that they name: `block_counts`: blocks live on each index of dp on entry; they sum to 256, and one index holds exactly 16. `block_dest`: for j < block_counts[s], the index of dp that receives block j of index s; every index receives exactly 4 blocks, no index sends more than 1 block to one index, and some index sends exactly 1 to one; entries with j >= block_counts[s] are unused. `factors`: each matrix is upper triangular with diagonal entries from 0.7 to 1.4.
All inputs are finite; a program needn't handle non-finite values.
Results may differ from a plain program's by a relative error of at most 0.003.
Values sent between devices are 32-bit elements; how exact they have to be, the bound alone decides.
A program may use at most 128 MiB of HBM per device.

v0:
```python
import math
import jax
import jax.numpy as jnp
from jax import lax
from jax.sharding import Mesh
from jax.sharding import PartitionSpec as P

K = 256
RB = 4
ITERS = 2
DP = ("dp_0", "dp_1", "dp_2")
DP_COMP = ("dp_0", "dp_1", "dp_2", "comp")
highest = lax.Precision.HIGHEST
ridge_term = 1.0
log_two_pi = math.log(2.0 * math.pi)


def laid_out(pieces, dim):
    pieces = jnp.moveaxis(pieces, 0, dim)
    dims = pieces.shape
    return pieces.reshape(*dims[:dim], dims[dim] * dims[dim + 1], *dims[dim + 2 :])


def stacked_from(value, axes, sequence):
    pieces = value[None]
    for k in sequence:
        pieces = lax.all_gather(pieces, axes[k], axis=0, tiled=True)
    block = [lax.axis_size(axes[k]) for k in reversed(sequence)]
    pieces = pieces.reshape(*block, *value.shape)
    turned = sorted(range(len(sequence)), key=lambda place: sequence[len(sequence) - 1 - place])
    return pieces.transpose(*turned, *range(len(sequence), pieces.ndim)).reshape(-1, *value.shape)


def gathered_by_axis(value, axes, sequence, dim):
    return laid_out(stacked_from(value, axes, sequence), dim)


def copy_for_each(value, axis):
    copies = jnp.broadcast_to(value, (lax.axis_size(axis), *value.shape))
    return lax.all_to_all(copies, axis, split_axis=0, concat_axis=0, tiled=True)


def gathered_once(value, axis):
    leaves = jax.tree.leaves(value)
    sequence = sorted(range(len(leaves)), key=lambda k: -leaves[k].size)
    width = (1, *leaves[sequence[0]].shape)[-1]
    lines = [
        jnp.pad(leaves[k].reshape(-1), (0, -leaves[k].size % width)).reshape(-1, width)
        for k in sequence
    ]
    both, at, found = (copy_for_each(jnp.concatenate(lines), axis), 0, {})
    for k, line in zip(sequence, lines):
        piece = both[:, at : at + len(line)].reshape(len(both), -1)
        found[k] = piece[:, : leaves[k].size].reshape(-1, *leaves[k].shape)
        at += len(line)
    numbers = iter(range(len(leaves)))
    return jax.tree.map(lambda _: found[next(numbers)], value)


def combined_pairwise(pieces, combine):
    while len(jax.tree.leaves(pieces)[0]) > 1:
        pieces = jax.vmap(combine)(
            *(jax.tree.map(lambda part: part[side::2], pieces) for side in (0, 1))
        )
    return jax.tree.map(lambda part: part[0], pieces)


def merged(value, axis, combine):
    pieces = gathered_once(value, axis)
    return combined_pairwise(pieces, combine)


def in_blocks(value, dim, size):
    before, after = (value.shape[:dim], value.shape[dim + 1 :])
    return jnp.moveaxis(value.reshape(*before, size, -1, *after), dim, 0)


def summed_on_arrival(value, axis, dim):
    size = lax.axis_size(axis)
    pieces = lax.all_to_all(in_blocks(value, dim, size), axis, 0, 0, tiled=True)
    return jnp.sum(pieces, axis=0)


def rebalance_rows(points, block_counts, block_dest):
    dp_devices = lax.axis_size(DP)
    dp_index = lax.axis_index(DP)
    nblocks = block_dest.shape[1]
    feature_width = points.shape[1]
    block_rows = points.shape[0] // nblocks
    slot_count = (nblocks + dp_devices - 1) // dp_devices
    blocks = points.reshape(nblocks, block_rows, feature_width)
    my_dest = lax.dynamic_index_in_dim(block_dest, dp_index, 0, keepdims=False)
    my_count = lax.dynamic_index_in_dim(block_counts, dp_index, 0, keepdims=False)
    positions = jnp.arange(nblocks, dtype=jnp.int32)
    targets = jnp.arange(dp_devices, dtype=jnp.int32)
    slot_ids = jnp.arange(slot_count, dtype=jnp.int32)
    send_hits = ((my_dest[:, None] == targets[None, :]) & (positions[:, None] < my_count)).astype(
        jnp.int32
    )
    send_rank = jnp.cumsum(send_hits, axis=0) - send_hits
    chosen = send_hits[:, :, None] * (send_rank[:, :, None] == slot_ids[None, None, :]).astype(
        jnp.int32
    )
    filled = jnp.sum(chosen, axis=0)
    source_block = jnp.sum(chosen * positions[:, None, None], axis=0)
    picked = jnp.take(blocks, source_block.reshape(-1), axis=0).reshape(
        dp_devices, slot_count, block_rows, feature_width
    )
    outgoing = jnp.where(filled[:, :, None, None] > 0, picked, 0.0)
    incoming = lax.all_to_all(outgoing, DP, split_axis=0, concat_axis=0, tiled=True)
    live_all = positions[None, :] < block_counts[:, None]
    sent_here = jnp.sum(((block_dest == dp_index) & live_all).astype(jnp.int32), axis=1)
    full_slot = (slot_ids[None, :] < sent_here[:, None]).astype(jnp.int32).reshape(-1)
    order_rank = jnp.cumsum(full_slot) - full_slot
    pick_slots = jnp.arange(RB, dtype=jnp.int32)
    pick_table = full_slot[None, :] * (order_rank[None, :] == pick_slots[:, None]).astype(jnp.int32)
    pick_index = jnp.sum(
        pick_table * jnp.arange(dp_devices * slot_count, dtype=jnp.int32)[None, :], axis=1
    )
    arrived = jnp.take(
        incoming.reshape(dp_devices * slot_count, block_rows, feature_width), pick_index, axis=0
    )
    return arrived.reshape(RB * block_rows, feature_width)


def densities(points_live, centres, factor_set, weights):
    members = centres.shape[0]
    group_width = math.gcd(members, 8)
    feature_width = centres.shape[1]

    def block_density(inputs):
        centre_set, factor_block, weight_block = inputs
        shifted = points_live[None, :, :] - centre_set[:, None, :]
        projected = jnp.einsum("grd,gde->gre", shifted, factor_block, precision=highest)
        logdet = jnp.sum(jnp.log(jnp.diagonal(factor_block, axis1=1, axis2=2)), axis=1)
        offset_terms = weight_block + logdet - 0.5 * feature_width * log_two_pi
        return offset_terms[:, None] - 0.5 * jnp.sum(projected * projected, axis=2)

    grouped = lax.map(
        block_density,
        (
            centres.reshape(members // group_width, group_width, feature_width),
            factor_set.reshape(members // group_width, group_width, feature_width, feature_width),
            weights.reshape(members // group_width, group_width),
        ),
    )
    return grouped.reshape(members, points_live.shape[0])


def moments(points_live, centres, responsibility):
    members = centres.shape[0]
    group_width = math.gcd(members, 8)
    feature_width = centres.shape[1]

    def block_moments(inputs):
        centre_set, weight_block = inputs
        shifted = points_live[None, :, :] - centre_set[:, None, :]
        weight_sum = jnp.sum(weight_block, axis=1)
        first_moment = jnp.einsum("gr,grd->gd", weight_block, shifted, precision=highest)
        second_moment = jnp.einsum(
            "grd,gre->gde", shifted * weight_block[:, :, None], shifted, precision=highest
        )
        return (weight_sum, first_moment, second_moment)

    weight_sums, firsts, seconds = lax.map(
        block_moments,
        (
            centres.reshape(members // group_width, group_width, feature_width),
            responsibility.reshape(members // group_width, group_width, responsibility.shape[1]),
        ),
    )
    return (
        weight_sums.reshape(members),
        firsts.reshape(members, feature_width),
        seconds.reshape(members, feature_width, feature_width),
    )


def pack_symmetric(matrix):
    half_width = matrix.shape[-1] // 2
    top_left = jnp.triu(matrix[:, :half_width, :half_width]) + jnp.tril(
        matrix[:, half_width:, half_width:], -1
    )
    packed = jnp.concatenate([top_left, matrix[:, :half_width, half_width:]], axis=2)
    corner = jnp.diagonal(matrix[:, half_width:, half_width:], axis1=1, axis2=2)
    return (packed, corner)


def unpack_symmetric(packed, corner):
    half_width = packed.shape[1]
    identity = jnp.eye(half_width, dtype=jnp.float32)
    top_left = packed[:, :, :half_width]
    right_block = packed[:, :, half_width:]
    first_block = jnp.triu(top_left) + jnp.swapaxes(jnp.triu(top_left, 1), 1, 2)
    strict_part = jnp.tril(top_left, -1)
    last_block = strict_part + jnp.swapaxes(strict_part, 1, 2) + corner[:, :, None] * identity
    upper_rows = jnp.concatenate([first_block, right_block], axis=2)
    lower_rows = jnp.concatenate([jnp.swapaxes(right_block, 1, 2), last_block], axis=2)
    return jnp.concatenate([upper_rows, lower_rows], axis=1)


def pack_upper(matrix):
    half_width = matrix.shape[-1] // 2
    top_left = matrix[:, :half_width, :half_width] + jnp.swapaxes(
        jnp.triu(matrix[:, half_width:, half_width:], 1), 1, 2
    )
    packed = jnp.concatenate([top_left, matrix[:, :half_width, half_width:]], axis=2)
    corner = jnp.diagonal(matrix[:, half_width:, half_width:], axis1=1, axis2=2)
    return (packed, corner)


def unpack_upper(packed, corner):
    half_width = packed.shape[1]
    identity = jnp.eye(half_width, dtype=jnp.float32)
    top_left = packed[:, :, :half_width]
    last_block = jnp.swapaxes(jnp.tril(top_left, -1), 1, 2) + corner[:, :, None] * identity
    upper_rows = jnp.concatenate([jnp.triu(top_left), packed[:, :, half_width:]], axis=2)
    lower_rows = jnp.concatenate([jnp.zeros_like(last_block), last_block], axis=2)
    return jnp.concatenate([upper_rows, lower_rows], axis=1)


def gathered_density(points_live, own_params):
    own_centres, own_factors, own_weights = own_params
    members = own_centres.shape[0] * lax.axis_size(DP)
    feature_width = own_centres.shape[1]
    initial = (
        jnp.zeros((members, points_live.shape[0]), jnp.float32),
        jnp.zeros((members, feature_width), jnp.float32),
    )
    packed, corner = pack_upper(own_factors)
    centre_piece = gathered_by_axis(own_centres, DP, (1, 0, 2), 0)
    offset = jnp.int32(0)
    log_table = lax.dynamic_update_slice_in_dim(
        initial[0],
        densities(
            points_live,
            centre_piece,
            unpack_upper(
                gathered_by_axis(packed, DP, (1, 0, 2), 0),
                gathered_by_axis(corner, DP, (1, 0, 2), 0),
            ),
            gathered_by_axis(own_weights, DP, (1, 0, 2), 0),
        ),
        offset,
        0,
    )
    centres = lax.dynamic_update_slice_in_dim(initial[1], centre_piece, offset, 0)
    return (log_table, centres)


def row_responsibility(log_table):
    row_peak = jnp.max(log_table, axis=0)
    row_scaled = jnp.sum(jnp.exp(log_table - row_peak[None, :]), axis=0)

    def combine(earlier, later):
        joint_peak = jnp.maximum(earlier[0], later[0])
        return (
            joint_peak,
            earlier[1] * jnp.exp(earlier[0] - joint_peak)
            + later[1] * jnp.exp(later[0] - joint_peak),
        )

    peak_all, scaled_all = merged((row_peak, row_scaled), "comp", combine)
    log_total = peak_all + jnp.log(scaled_all)
    return (log_total, jnp.exp(log_table - log_total[None, :]))


def summed_moments(statistics):
    weight_sum, first_moment, second_moment = statistics
    packed, corner = pack_symmetric(second_moment)
    totals = (
        summed_on_arrival(weight_sum, DP, 0),
        summed_on_arrival(first_moment, DP, 0),
        summed_on_arrival(packed, DP, 0),
        summed_on_arrival(corner, DP, 0),
    )
    return (totals[0], totals[1], unpack_symmetric(totals[2], totals[3]))


def refresh(centres, weight_sum, first_moment, second_moment, total_points):
    identity = jnp.eye(centres.shape[1], dtype=jnp.float32)
    counted = weight_sum + 1.0
    covariance = (
        second_moment
        - first_moment[:, :, None] * first_moment[:, None, :] / counted[:, None, None]
        + ridge_term * identity
    ) / counted[:, None, None]
    cholesky_lower = jnp.linalg.cholesky(covariance)
    inverse_lower = jax.scipy.linalg.solve_triangular(
        cholesky_lower, jnp.broadcast_to(identity, covariance.shape), lower=True
    )
    return (
        centres + first_moment / counted[:, None],
        jnp.swapaxes(inverse_lower, 1, 2),
        jnp.log(counted / total_points),
    )


def per_device(points, block_counts, block_dest, means, factors, log_weights):
    points_live = rebalance_rows(points, block_counts, block_dest)
    total_points = float(lax.axis_size(DP) * points_live.shape[0] + K)
    current = (means, factors, log_weights)
    for iteration in range(ITERS):
        log_table, centres = gathered_density(points_live, current)
        log_total, responsibility = row_responsibility(log_table)
        weight_sum, first_moment, second_moment = summed_moments(
            moments(points_live, centres, responsibility)
        )
        current = refresh(current[0], weight_sum, first_moment, second_moment, total_points)
    new_means, new_factors, new_weights = current
    return (new_means, new_factors, new_weights, log_total / points.shape[1])


def solution(mesh):
    split = Mesh(
        mesh.devices.reshape(8, 4, 2, mesh.shape["comp"]), ("dp_0", "dp_1", "dp_2", "comp")
    )
    in_specs = (P(DP, None), P(), P(), P(DP_COMP, None), P(DP_COMP, None, None), P(DP_COMP))
    out_specs = (P(DP_COMP, None), P(DP_COMP, None, None), P(DP_COMP), P(DP))
    return jax.shard_map(
        per_device, mesh=split, in_specs=in_specs, out_specs=out_specs, check_vma=False
    )
```

profile of v0, /device:TPU:8, one launch (start us, length us, event | category | flops | bytes accessed | tf_op | source)
XLA Modules:
  0.0 927.8 jit_solution(11059183866429565092)
XLA Ops:
  9.2 13.0 %all-gather.3 = f32[4,64,128]{2,1,0:T(8,128)} all-gather(f32[1,64,128]{2,1,0:T(8,128)S(1)} %copy.268), channel_id=5, replica_groups=mesh['dp_0'=8,'dp_1'=4,'dp_2'=2,'comp'=4] {'dp_1'}, dimensions={0}, use_global_device_ids=true | all-gather | bytes 163840 | tf_op jit(solution)/shard_map/all_gather | solution.py:27
  27.6 12.0 %all-to-all-start = ((f32[64,1,64,128]{3,2,1,0:T(8,128)}), f32[64,1,64,128]{3,2,1,0:T(8,128)}, u32[]{:S(2)}, u32[]{:S(2)}) async-start(f32[64,1,64,128]{3,2,1,0:T(8,128)} %fusion.48), calls=%async_computation | async-start | bytes 4194304 | tf_op jit(solution)/shard_map/all_to_all | solution.py:110
  39.7 34.5 %all-gather.26.cloned.1.call-done = f32[32,64,128]{2,1,0:T(8,128)} async-done(((f32[4,64,128]{2,1,0:T(8,128)}), f32[32,64,128]{2,1,0:T(8,128)}) %all-gather.26.cloned.1.call-update) | async-done | bytes 1048592 | tf_op jit(solution)/shard_map/all_gather | solution.py:27
  78.0 9.6 %all-reduce.11 = (f32[4]{0:T(128)S(1)}, f32[256]{0:T(256)S(1)}) all-reduce(f32[4]{0:T(128)S(1)} %dynamic-update-slice.2, f32[256]{0:T(256)S(1)} %dynamic-update-slice.5), channel_id=2, replica_groups=mesh['dp_0'=8,'dp_1'=4,'dp_2'=2,'comp'=4] {'dp_1'}, use_global_device_ids=true, to_apply=%add.2 | all-reduce | flops 260 | bytes 2080
  88.0 24.3 %all_gather.79 = f32[32,1,64]{2,1,0:T(1,128)S(1)} all-gather(f32[4,1,64]{2,1,0:T(1,128)S(1)} %reshape.913), channel_id=1, replica_groups=mesh['dp_0'=8,'dp_1'=4,'dp_2'=2,'comp'=4] {'dp_0'}, dimensions={0}, use_global_device_ids=true | all-gather | bytes 9216 | tf_op jit(solution)/shard_map/all_gather | solution.py:27
  117.3 14.4 %all-reduce.3 = f32[32]{0:T(128)S(1)} all-reduce(f32[32]{0:T(128)S(1)} %dynamic-update-slice.3), channel_id=3, replica_groups=mesh['dp_0'=8,'dp_1'=4,'dp_2'=2,'comp'=4] {'dp_0'}, use_global_device_ids=true, to_apply=%add.3 | all-reduce | flops 32 | bytes 256
  134.6 8.4 all-gather.17
  143.0 22.2 %all-gather.18 = f32[8,4,128]{2,1,0:T(4,128)S(1)} all-gather(f32[1,4,128]{2,1,0:T(4,128)S(1)} %bitcast.330), channel_id=10, replica_groups=mesh['dp_0'=8,'dp_1'=4,'dp_2'=2,'comp'=4] {'dp_0'}, dimensions={0}, use_global_device_ids=true | all-gather | bytes 18432 | tf_op jit(solution)/shard_map/all_gather | solution.py:27
  186.9 7.4 copy.337
  196.5 92.3 %while.52 = (s32[]{:T(128)}, f32[8,8,256]{2,1,0:T(8,128)S(1)}, f32[8,8]{1,0:T(8,128)S(1)}, f32[8,8,128,128]{2,3,1,0:T(8,128)}, f32[4,64,128]{2,1,0:T(8,128)S(1)}, /*index=5*/f32[8,8,128]{2,1,0:T(8,128)S(1)}, s32[]{:T(128)}) while((s32[]{:T(128)}, f32[8,8,256]{2,1,0:T(8,128)S(1)}, f32[8,8]{1,0:T(8,128)S(1)}, f32[8,8,128,128]{2,3,1,0:T(8,128)}, ...), condition=%wide.region_9.10_spmd, body=%wide.region_6.9_spmd.sunk | while | flops 403443200 | bytes 2803933 | solution.py:139
  198.8 7.4 copy.392
  210.3 7.4 copy.392
  221.8 7.4 copy.392
  233.4 7.4 copy.392
  244.9 7.4 copy.392
  256.4 7.4 copy.392
  268.0 7.4 copy.392
  279.5 7.4 copy.392
  302.6 31.7 %while.53 = (s32[]{:T(128)}, f32[8,8]{1,0:T(8,128)S(1)}, f32[8,8,128]{2,1,0:T(8,128)}, f32[8,8,128,128]{3,2,1,0:T(8,128)}, f32[8,8,256]{2,1,0:T(8,128)S(1)}, /*i...) while((s32[]{:T(128)}, f32[8,8]{1,0:T(8,128)S(1)}, ...), condition=%wide.region_14.15_spmd, body=%wide.region_12.14_spmd.sunk | while | flops 406849536 | bytes 1254601 | solution.py:165
  354.2 10.3 %all-to-all-start.5 = ((f32[64,1,64]{2,1,0:T(1,128)}), f32[64,1,64]{2,1,0:T(1,128)S(1)}, u32[]{:S(2)}, u32[]{:S(2)}) async-start(f32[64,1,64]{2,1,0:T(1,128)} %copy.297), calls=%async_computation.5 | async-start | bytes 65536 | tf_op jit(solution)/shard_map/all_to_all | solution.py:80
  373.1 9.3 %all-to-all-start.2 = ((f32[64,1,128]{2,1,0:T(1,128)}), f32[64,1,128]{2,1,0:T(1,128)S(1)}, u32[]{:S(2)}, u32[]{:S(2)}) async-start(f32[64,1,128]{2,1,0:T(1,128)} %bitcast.68), calls=%async_computation.2 | async-start | bytes 65536 | tf_op jit(solution)/shard_map/all_to_all | solution.py:80
  391.0 9.9 %all-to-all-start.4 = ((f32[64,1,64,128]{3,2,1,0:T(8,128)}), f32[64,1,64,128]{3,2,1,0:T(8,128)S(1)}, u32[]{:S(2)}, u32[]{:S(2)}) async-start(f32[64,1,64,128]{3,2,1,0:T(8,128)} %copy.291), calls=%async_computation.4 | async-start | bytes 4194304 | tf_op jit(solution)/shard_map/all_to_all | solution.py:80
  402.9 49.3 %all-to-all-done.4 = f32[64,1,64,128]{3,2,1,0:T(8,128)S(1)} async-done(((f32[64,1,64,128]{3,2,1,0:T(8,128)}), f32[64,1,64,128]{3,2,1,0:T(8,128)S(1)}, u32[]{:S(2)}, u32[]{:S(2)}) %all-to-all-start.4) | async-done | bytes 2097184 | tf_op jit(solution)/shard_map/all_to_all | solution.py:80
  452.9 11.7 %custom-call.20 = f32[1,128,128]{2,1,0:T(8,128)S(1)} custom-call(f32[1,128,128]{2,1,0:T(8,128)S(1)} %fusion.54), custom_call_target="Cholesky" | custom-call | tf_op jit(solution)/shard_map/jit(cholesky)/cholesky | solution.py:288
  466.0 9.8 %custom-call.21 = f32[1,128,128]{1,2,0:T(8,128)S(1)} custom-call(f32[1,128,128]{2,1,0:T(8,128)S(1)} %select_select_fusion.1), custom_call_target="InvertDiagBlocksLowerTriangular" | custom-call | tf_op jit(solution)/shard_map/jit(_solve_triangular)/triangular_solve | solution.py:289
  476.4 12.8 %all-gather.10 = f32[4,64,128]{2,1,0:T(8,128)} all-gather(f32[1,64,128]{2,1,0:T(8,128)S(1)} %copy.302), channel_id=12, replica_groups=mesh['dp_0'=8,'dp_1'=4,'dp_2'=2,'comp'=4] {'dp_1'}, dimensions={0}, use_global_device_ids=true | all-gather | bytes 163840 | tf_op jit(solution)/shard_map/all_gather | solution.py:27
  489.3 32.6 %all-gather.30.cloned.1.call-done = f32[32,64,128]{2,1,0:T(8,128)} async-done(((f32[4,64,128]{2,1,0:T(8,128)}), f32[32,64,128]{2,1,0:T(8,128)}) %all-gather.30.cloned.1.call-update) | async-done | bytes 1048592 | tf_op jit(solution)/shard_map/all_gather | solution.py:27
  522.7 7.8 all-gather.19
  530.5 21.2 %all-gather.20 = f32[8,4,128]{2,1,0:T(4,128)S(1)} all-gather(f32[1,4,128]{2,1,0:T(4,128)S(1)} %bitcast.331), channel_id=17, replica_groups=mesh['dp_0'=8,'dp_1'=4,'dp_2'=2,'comp'=4] {'dp_0'}, dimensions={0}, use_global_device_ids=true | all-gather | bytes 18432 | tf_op jit(solution)/shard_map/all_gather | solution.py:27
  554.6 10.1 %all-reduce.10 = (f32[4]{0:T(128)S(1)}, f32[256]{0:T(256)S(1)}) all-reduce(f32[4]{0:T(128)S(1)} %dynamic-update-slice.6, f32[256]{0:T(256)S(1)} %dynamic-update-slice.9), channel_id=1, replica_groups=mesh['dp_0'=8,'dp_1'=4,'dp_2'=2,'comp'=4] {'dp_1'}, use_global_device_ids=true, to_apply=%add.6 | all-reduce | flops 260 | bytes 2080
  564.9 21.5 %all_gather.91 = f32[32,1,64]{2,1,0:T(1,128)S(1)} all-gather(f32[4,1,64]{2,1,0:T(1,128)S(1)} %reshape.920), channel_id=1, replica_groups=mesh['dp_0'=8,'dp_1'=4,'dp_2'=2,'comp'=4] {'dp_0'}, dimensions={0}, use_global_device_ids=true | all-gather | bytes 9216 | tf_op jit(solution)/shard_map/all_gather | solution.py:27
  588.5 15.4 %all-reduce.7 = f32[32]{0:T(128)S(1)} all-reduce(f32[32]{0:T(128)S(1)} %dynamic-update-slice.7), channel_id=1, replica_groups=mesh['dp_0'=8,'dp_1'=4,'dp_2'=2,'comp'=4] {'dp_0'}, use_global_device_ids=true, to_apply=%add.7 | all-reduce | flops 32 | bytes 256
  638.8 92.3 %while.54 = (s32[]{:T(128)}, f32[8,8,256]{2,1,0:T(8,128)S(1)}, f32[8,8]{1,0:T(8,128)S(1)}, f32[8,8,128,128]{2,3,1,0:T(8,128)}, f32[4,64,128]{2,1,0:T(8,128)S(1)}, /*index=5*/f32[8,8,128]{2,1,0:T(8,128)S(1)}, s32[]{:T(128)}) while((s32[]{:T(128)}, f32[8,8,256]{2,1,0:T(8,128)S(1)}, f32[8,8]{1,0:T(8,128)S(1)}, f32[8,8,128,128]{2,3,1,0:T(8,128)}, ...), condition=%wide.region_24.27_spmd, body=%wide.region_21.26_spmd.sunk | while | flops 403443200 | bytes 2803933 | solution.py:139
  641.1 7.4 copy.395
  652.6 7.4 copy.395
  664.1 7.4 copy.395
  675.7 7.4 copy.395
  687.2 7.4 copy.395
  698.7 7.4 copy.395
  710.3 7.4 copy.395
  721.8 7.4 copy.395
  745.4 31.7 %while.55 = (s32[]{:T(128)}, f32[8,8]{1,0:T(8,128)S(1)}, f32[8,8,128]{2,1,0:T(8,128)}, f32[8,8,128,128]{3,2,1,0:T(8,128)}, f32[8,8,256]{2,1,0:T(8,128)S(1)}, /*i...) while((s32[]{:T(128)}, f32[8,8]{1,0:T(8,128)S(1)}, ...), condition=%wide.region_29.32_spmd, body=%wide.region_27.31_spmd.sunk | while | flops 406849536 | bytes 1254601 | solution.py:165
  797.0 10.3 %all-to-all-start.10 = ((f32[64,1,64]{2,1,0:T(1,128)}), f32[64,1,64]{2,1,0:T(1,128)S(1)}, u32[]{:S(2)}, u32[]{:S(2)}) async-start(f32[64,1,64]{2,1,0:T(1,128)} %copy.327), calls=%async_computation.10 | async-start | bytes 65536 | tf_op jit(solution)/shard_map/all_to_all | solution.py:80
  815.9 9.3 %all-to-all-start.7 = ((f32[64,1,128]{2,1,0:T(1,128)}), f32[64,1,128]{2,1,0:T(1,128)S(1)}, u32[]{:S(2)}, u32[]{:S(2)}) async-start(f32[64,1,128]{2,1,0:T(1,128)} %bitcast.109), calls=%async_computation.7 | async-start | bytes 65536 | tf_op jit(solution)/shard_map/all_to_all | solution.py:80
  833.8 10.3 %all-to-all-start.9 = ((f32[64,1,64,128]{3,2,1,0:T(8,128)}), f32[64,1,64,128]{3,2,1,0:T(8,128)S(1)}, u32[]{:S(2)}, u32[]{:S(2)}) async-start(f32[64,1,64,128]{3,2,1,0:T(8,128)} %copy.321), calls=%async_computation.9 | async-start | bytes 4194304 | tf_op jit(solution)/shard_map/all_to_all | solution.py:80
  846.2 49.0 %all-to-all-done.9 = f32[64,1,64,128]{3,2,1,0:T(8,128)S(1)} async-done(((f32[64,1,64,128]{3,2,1,0:T(8,128)}), f32[64,1,64,128]{3,2,1,0:T(8,128)S(1)}, u32[]{:S(2)}, u32[]{:S(2)}) %all-to-all-start.9) | async-done | bytes 2097184 | tf_op jit(solution)/shard_map/all_to_all | solution.py:80
  896.0 11.7 %custom-call.22 = f32[1,128,128]{2,1,0:T(8,128)S(1)} custom-call(f32[1,128,128]{2,1,0:T(8,128)S(1)} %fusion.52), custom_call_target="Cholesky" | custom-call | tf_op jit(solution)/shard_map/jit(cholesky)/cholesky | solution.py:288
  909.0 9.8 %custom-call.23 = f32[1,128,128]{1,2,0:T(8,128)S(1)} custom-call(f32[1,128,128]{2,1,0:T(8,128)S(1)} %select_select_fusion), custom_call_target="InvertDiagBlocksLowerTriangular" | custom-call | tf_op jit(solution)/shard_map/jit(_solve_triangular)/triangular_solve | solution.py:289
  (476 shorter events, 320.9 us)
Async XLA Ops:
  7.2 18.1 %copy-start = (f32[1024,128]{1,0:T(8,128)S(1)}, f32[1024,128]{1,0:T(8,128)}, u32[]{:S(2)}) copy-start(f32[1024,128]{1,0:T(8,128)} %param.17) | copy-start | bytes 1572868
  7.2 67.0 %all-gather.26.cloned.1.call-start = ((), (), s32[]{:S(2)}) async-start(), calls=%async_computation.11 | async-start | bytes 1179648 | tf_op jit(solution)/shard_map/all_gather | solution.py:27
  27.6 47.3 %copy-start.10 = (u32[256]{0:T(256)S(1)}, u32[256]{0:T(256)}, u32[]{:S(2)}) copy-start(u32[256]{0:T(256)} %constant.370) | copy-start | bytes 3076
  27.6 59.9 %copy-start.5 = (s32[64,16]{0,1:T(8,128)S(1)}, s32[64,16]{0,1:T(8,128)}, u32[]{:S(2)}) copy-start(s32[64,16]{0,1:T(8,128)} %param.19) | copy-start | bytes 12292
  27.6 59.9 %copy-start.7 = (s32[64]{0:T(128)S(1)}, s32[64]{0:T(128)}, u32[]{:S(2)}) copy-start(s32[64]{0:T(128)} %param.18) | copy-start | bytes 772
  27.6 86.8 %copy-start.9 = (u32[256]{0:T(256)S(1)}, u32[256]{0:T(256)}, u32[]{:S(2)}) copy-start(u32[256]{0:T(256)} %constant.375) | copy-start | bytes 3076
  27.6 87.4 %copy-start.8 = (u32[256]{0:T(256)S(1)}, u32[256]{0:T(256)}, u32[]{:S(2)}) copy-start(u32[256]{0:T(256)} %constant.380) | copy-start | bytes 3076
  27.6 107.0 %copy-start.6 = (f32[1,128]{1,0:T(1,128)S(1)}, f32[1,128]{1,0:T(1,128)}, u32[]{:S(2)}) copy-start(f32[1,128]{1,0:T(1,128)} %param.20) | copy-start | bytes 1540
  27.6 166.7 %all-to-all-start = ((f32[64,1,64,128]{3,2,1,0:T(8,128)}), f32[64,1,64,128]{3,2,1,0:T(8,128)}, u32[]{:S(2)}, u32[]{:S(2)}) async-start(f32[64,1,64,128]{3,2,1,0:T(8,128)} %fusion.48), calls=%async_computation | async-start | bytes 4194304 | tf_op jit(solution)/shard_map/all_to_all | solution.py:110
  39.7 127.8 %all-gather.28.cloned.1.call-start = ((), (), s32[]{:S(2)}) async-start(), calls=%async_computation.12 | async-start | bytes 3145728 | tf_op jit(solution)/shard_map/all_gather | solution.py:27
  289.5 9.8 %all-to-all-start.1 = ((f32[4,2,256]{2,1,0:T(2,128)}), f32[4,2,256]{2,1,0:T(2,128)S(1)}, u32[]{:S(2)}, u32[]{:S(2)}) async-start(f32[4,2,256]{2,1,0:T(2,128)} %broadcast_in_dim.229), calls=%async_computation.1 | async-start | bytes 16384 | tf_op jit(solution)/shard_map/all_to_all | solution.py:40
  335.0 19.2 %all-to-all-start.3 = ((f32[64,1,1]{2,1,0:T(1,128)}), f32[64,1,1]{2,1,0:T(1,128)S(1)}, u32[]{:S(2)}, u32[]{:S(2)}) async-start(f32[64,1,1]{2,1,0:T(1,128)} %all_to_all.52), calls=%async_computation.3 | async-start | bytes 65536 | tf_op jit(solution)/shard_map/all_to_all | solution.py:80
  354.2 18.9 %all-to-all-start.5 = ((f32[64,1,64]{2,1,0:T(1,128)}), f32[64,1,64]{2,1,0:T(1,128)S(1)}, u32[]{:S(2)}, u32[]{:S(2)}) async-start(f32[64,1,64]{2,1,0:T(1,128)} %copy.297), calls=%async_computation.5 | async-start | bytes 65536 | tf_op jit(solution)/shard_map/all_to_all | solution.py:80
  368.7 13.8 %copy-start.4 = (f32[64,64,64]{0,2,1:T(8,128)S(1)}, f32[64,64,64]{0,2,1:T(8,128)}, u32[]{:S(2)}) copy-start(f32[64,64,64]{0,2,1:T(8,128)} %select_add_fusion.1) | copy-start | bytes 3145732
  373.1 17.9 %all-to-all-start.2 = ((f32[64,1,128]{2,1,0:T(1,128)}), f32[64,1,128]{2,1,0:T(1,128)S(1)}, u32[]{:S(2)}, u32[]{:S(2)}) async-start(f32[64,1,128]{2,1,0:T(1,128)} %bitcast.68), calls=%async_computation.2 | async-start | bytes 65536 | tf_op jit(solution)/shard_map/all_to_all | solution.py:80
  391.0 61.1 %all-to-all-start.4 = ((f32[64,1,64,128]{3,2,1,0:T(8,128)}), f32[64,1,64,128]{3,2,1,0:T(8,128)S(1)}, u32[]{:S(2)}, u32[]{:S(2)}) async-start(f32[64,1,64,128]{3,2,1,0:T(8,128)} %copy.291), calls=%async_computation.4 | async-start | bytes 4194304 | tf_op jit(solution)/shard_map/all_to_all | solution.py:80
  400.9 120.9 %all-gather.30.cloned.1.call-start = ((), (), s32[]{:S(2)}) async-start(), calls=%async_computation.13 | async-start | bytes 1179648 | tf_op jit(solution)/shard_map/all_gather | solution.py:27
  489.2 117.8 %all-gather.32.cloned.1.call-start = ((), (), s32[]{:S(2)}) async-start(), calls=%async_computation.14 | async-start | bytes 3145728 | tf_op jit(solution)/shard_map/all_gather | solution.py:27
  622.3 3.4 copy-start.2
  731.8 9.8 %all-to-all-start.6 = ((f32[4,2,256]{2,1,0:T(2,128)}), f32[4,2,256]{2,1,0:T(2,128)S(1)}, u32[]{:S(2)}, u32[]{:S(2)}) async-start(f32[4,2,256]{2,1,0:T(2,128)} %broadcast_in_dim.234), calls=%async_computation.6 | async-start | bytes 16384 | tf_op jit(solution)/shard_map/all_to_all | solution.py:40
  777.8 19.2 %all-to-all-start.8 = ((f32[64,1,1]{2,1,0:T(1,128)}), f32[64,1,1]{2,1,0:T(1,128)S(1)}, u32[]{:S(2)}, u32[]{:S(2)}) async-start(f32[64,1,1]{2,1,0:T(1,128)} %all_to_all.53), calls=%async_computation.8 | async-start | bytes 65536 | tf_op jit(solution)/shard_map/all_to_all | solution.py:80
  797.0 18.9 %all-to-all-start.10 = ((f32[64,1,64]{2,1,0:T(1,128)}), f32[64,1,64]{2,1,0:T(1,128)S(1)}, u32[]{:S(2)}, u32[]{:S(2)}) async-start(f32[64,1,64]{2,1,0:T(1,128)} %copy.327), calls=%async_computation.10 | async-start | bytes 65536 | tf_op jit(solution)/shard_map/all_to_all | solution.py:80
  811.5 13.8 %copy-start.3 = (f32[64,64,64]{0,2,1:T(8,128)S(1)}, f32[64,64,64]{0,2,1:T(8,128)}, u32[]{:S(2)}) copy-start(f32[64,64,64]{0,2,1:T(8,128)} %select_add_fusion) | copy-start | bytes 3145732
  815.9 17.9 %all-to-all-start.7 = ((f32[64,1,128]{2,1,0:T(1,128)}), f32[64,1,128]{2,1,0:T(1,128)S(1)}, u32[]{:S(2)}, u32[]{:S(2)}) async-start(f32[64,1,128]{2,1,0:T(1,128)} %bitcast.109), calls=%async_computation.7 | async-start | bytes 65536 | tf_op jit(solution)/shard_map/all_to_all | solution.py:80
  833.8 61.4 %all-to-all-start.9 = ((f32[64,1,64,128]{3,2,1,0:T(8,128)}), f32[64,1,64,128]{3,2,1,0:T(8,128)S(1)}, u32[]{:S(2)}, u32[]{:S(2)}) async-start(f32[64,1,64,128]{3,2,1,0:T(8,128)} %copy.321), calls=%async_computation.9 | async-start | bytes 4194304 | tf_op jit(solution)/shard_map/all_to_all | solution.py:80
  844.1 75.8 %copy-start.1 = (f32[1024,128]{1,0:T(8,128)S(1)}, f32[1024,128]{1,0:T(8,128)}, u32[]{:S(2)}) copy-start(f32[1024,128]{1,0:T(8,128)} %param.17) | copy-start | bytes 1572868
Sparse Core Ops, SparseCore 0:
  22.3 51.8 all-gather.25
  76.0 15.5 all-gather.27
  489.3 32.4 all-gather.29
  523.5 14.2 all-gather.31
where the time goes:
time: 934 us; the launch traced here: 928 us
  local copies, waits for them, and re-layouts  279 us (30%)
  blocking collectives  193 us (21%)
  waiting for transfers between devices  179 us (19%)
  starting transfers between devices  94.7 us (10%)
  other arithmetic  93.8 us (10%)
  matrix products  68 us (7%)
  between operations  19.9 us (2%)
    all_gather x12, blocking collectives, stacked_from(): pieces = lax.all_gather(pieces, axes[k], axis=0, tiled=True)  139 us
    squeeze x32, local copies, waits for them, and re-layouts, densities(): lax.map(block_density, (centres.reshape(members // group_width, group_wid...  135 us
    all_to_all x8, waiting for transfers between devices, summed_on_arrival(): pieces = lax.all_to_all(in_blocks(value, dim, size), axis, 0, 0, tiled=True)  101 us
    all_to_all x8, starting transfers between devices, summed_on_arrival(): pieces = lax.all_to_all(in_blocks(value, dim, size), axis, 0, 0, tiled=True)  73.2 us
    all_gather x4, waiting for transfers between devices, stacked_from(): pieces = lax.all_gather(pieces, axes[k], axis=0, tiled=True)  67.1 us
    unnamed x6, blocking collectives  54.6 us
    unnamed x59, local copies, waits for them, and re-layouts  35.6 us
    dot_general x16, matrix products, block_moments(): jnp.einsum('grd,gre->gde', shifted * weight_block[:, :, None], shifted, p...  33.4 us
  transfers between devices with their start and end apart: 15, of which 10 were waited for; matrix products, arithmetic and copies ran while one was open for 11% of the time, Pallas kernels for 0%

commit v1 on v0

--- a/solution.py
+++ b/solution.py
@@ -24,7 +24,9 @@
 def stacked_from(value, axes, sequence):
     pieces = value[None]
     for k in sequence:
-        pieces = lax.all_gather(pieces, axes[k], axis=0, tiled=True)
+        pieces = jnp.concatenate(
+            lax.all_to_all(jnp.stack([pieces] * lax.axis_size(axes[k])), axes[k], 0, 0), axis=0
+        )
     block = [lax.axis_size(axes[k]) for k in reversed(sequence)]
     pieces = pieces.reshape(*block, *value.shape)
     turned = sorted(range(len(sequence)), key=lambda place: sequence[len(sequence) - 1 - place])

time: 934 us -> 900 us (0.964)
  blocking collectives: 193 us -> 65.1 us
  waiting for transfers between devices: 179 us -> 231 us
  starting transfers between devices: 94.7 us -> 139 us
  between operations: 19.9 us -> 4.91 us
  other arithmetic: 93.8 us -> 104 us
    all_gather x12 -> x0, blocking collectives: 139 us -> none  [stacked_from(): pieces = lax.all_gather(pieces, axes[k], axis=0, tiled=True)]
    all_to_all x0 -> x15, waiting for transfers between devices: none -> 88.9 us  [stacked_from(): lax.all_to_all(jnp.stack([pieces] * lax.axis_size(axes[k])), axes[k], 0, 0)]
    all_gather x4 -> x0, waiting for transfers between devices: 67.1 us -> none  [stacked_from(): pieces = lax.all_gather(pieces, axes[k], axis=0, tiled=True)]
    all_to_all x0 -> x15, starting transfers between devices: none -> 66.5 us  [stacked_from(): lax.all_to_all(jnp.stack([pieces] * lax.axis_size(axes[k])), axes[k], 0, 0)]
    all_to_all x0 -> x10, blocking collectives: none -> 65.1 us  [the longest x9 51.3 us: stacked_from(): lax.all_to_all(jnp.stack([pieces] * lax.axis_size(axes[k])), axes[k], 0, 0)]
    unnamed x6 -> x0, blocking collectives: 54.6 us -> none
    all_to_all x1, waiting for transfers between devices: 0.01 us -> 23.2 us  [rebalance_rows(): lax.all_to_all(outgoing, DP, split_axis=0, concat_axis=0, tiled=True)]
    all_to_all x8 -> x7, starting transfers between devices: 73.2 us -> 57.4 us  [summed_on_arrival(): pieces = lax.all_to_all(in_blocks(value, dim, size), axis, 0, 0, tiled=True)]
  transfers between devices with their start and end apart: 15 -> 25, of which waited for: 10 -> 20; matrix products, arithmetic and copies ran while one was open for 11% -> 12% of each run, Pallas kernels for 0% -> 0%
where the time goes in v1:
time: 900 us; the launch traced here: 892 us
  local copies, waits for them, and re-layouts  280 us (31%)
  waiting for transfers between devices  231 us (26%)
  starting transfers between devices  139 us (15%)
  other arithmetic  104 us (12%)
  matrix products  68 us (8%)
  blocking collectives  65.1 us (7%)
    squeeze x32, local copies, waits for them, and re-layouts, densities(): lax.map(block_density, (centres.reshape(members // group_width, group_wid...  135 us
    all_to_all x7, waiting for transfers between devices, summed_on_arrival(): pieces = lax.all_to_all(in_blocks(value, dim, size), axis, 0, 0, tiled=True)  109 us
    all_to_all x15, waiting for transfers between devices, stacked_from(): lax.all_to_all(jnp.stack([pieces] * lax.axis_size(axes[k])), axes[k], 0, 0)  88.9 us
    all_to_all x15, starting transfers between devices, stacked_from(): lax.all_to_all(jnp.stack([pieces] * lax.axis_size(axes[k])), axes[k], 0, 0)  66.5 us
    all_to_all x7, starting transfers between devices, summed_on_arrival(): pieces = lax.all_to_all(in_blocks(value, dim, size), axis, 0, 0, tiled=True)  57.4 us
    all_to_all x9, blocking collectives, stacked_from(): lax.all_to_all(jnp.stack([pieces] * lax.axis_size(axes[k])), axes[k], 0, 0)  51.3 us
    dot_general x16, matrix products, block_moments(): jnp.einsum('grd,gre->gde', shifted * weight_block[:, :, None], shifted, p...  33.3 us
    unnamed x44, local copies, waits for them, and re-layouts  32.7 us
  transfers between devices with their start and end apart: 25, of which 20 were waited for; matrix products, arithmetic and copies ran while one was open for 12% of the time, Pallas kernels for 0%

profile of v1, /device:TPU:8, one launch (start us, length us, event | category | flops | bytes accessed | tf_op | source)
XLA Modules:
  0.0 892.5 jit_solution(5718596401190499203)
XLA Ops:
  11.8 8.0 all-to-all-start.1
  20.6 6.8 all-to-all-done.1
  50.4 6.7 all-to-all-done.7
  61.2 7.6 all-to-all-done.11
  68.8 8.2 all_to_all.185
  89.6 13.7 %all-to-all-done.4 = f32[8,4,1,64,128]{4,3,1,2,0:T(8,128)} async-done(((f32[8,4,1,64,128]{4,3,1,2,0:T(8,128)}), f32[8,4,1,64,128]{4,3,1,2,0:T(8,128)}, u32[]{:S(2)}, u32[]{:S(2)}) %all-to-all-start.4) | async-done | bytes 1048608 | tf_op jit(solution)/shard_map/all_to_all | solution.py:28
  117.1 6.6 all_to_all.188
  123.7 6.7 all-to-all-start.9
  150.9 7.4 copy.329
  158.3 23.2 %all-to-all-done.9 = f32[64,1,64,128]{3,2,1,0:T(8,128)} async-done(((f32[64,1,64,128]{3,2,1,0:T(8,128)}), f32[64,1,64,128]{3,2,1,0:T(8,128)}, u32[]{:S(2)}, u32[]{:S(2)}) %all-to-all-start.9) | async-done | bytes 2097184 | tf_op jit(solution)/shard_map/all_to_all | solution.py:112
  183.8 92.3 %while.52 = (s32[]{:T(128)}, f32[8,8,256]{2,1,0:T(8,128)S(1)}, f32[8,8]{1,0:T(8,128)S(1)}, f32[8,8,128,128]{2,3,1,0:T(8,128)}, f32[4,64,128]{2,1,0:T(8,128)S(1)}, /*index=5*/f32[8,8,128]{2,1,0:T(8,128)S(1)}, s32[]{:T(128)}) while((s32[]{:T(128)}, f32[8,8,256]{2,1,0:T(8,128)S(1)}, f32[8,8]{1,0:T(8,128)S(1)}, f32[8,8,128,128]{2,3,1,0:T(8,128)}, ...), condition=%wide.region_9.10_spmd, body=%wide.region_6.9_spmd.sunk | while | flops 403443200 | bytes 2803933 | solution.py:141
  186.0 7.4 copy.384
  197.5 7.4 copy.384
  209.1 7.4 copy.384
  220.6 7.4 copy.384
  232.2 7.4 copy.384
  243.7 7.4 copy.384
  255.2 7.4 copy.384
  266.8 7.4 copy.384
  289.8 31.7 %while.53 = (s32[]{:T(128)}, f32[8,8]{1,0:T(8,128)S(1)}, f32[8,8,128]{2,1,0:T(8,128)}, f32[8,8,128,128]{3,2,1,0:T(8,128)}, f32[8,8,256]{2,1,0:T(8,128)S(1)}, /*i...) while((s32[]{:T(128)}, f32[8,8]{1,0:T(8,128)S(1)}, ...), condition=%wide.region_14.15_spmd, body=%wide.region_12.14_spmd.sunk | while | flops 406849536 | bytes 1254601 | solution.py:167
  321.6 13.9 %all_to_all.194 = f32[64,1,1]{2,1,0:T(1,128)S(1)} all-to-all(f32[64,1,1]{2,1,0:T(1,128)S(1)} %all_to_all.148), channel_id=1, replica_groups=mesh['dp_0'=8,'dp_1'=4,'dp_2'=2,'comp'=4] {'dp_0','dp_1','dp_2'}, dimensions={0} | all-to-all | bytes 512 | tf_op jit(solution)/shard_map/all_to_all | solution.py:82
  336.9 7.6 all_to_all.189
  361.5 6.9 all-to-all-start.17
  381.5 8.5 all-to-all-done.20
  415.1 11.2 %all-to-all-start.19 = ((f32[64,1,64,128]{3,2,1,0:T(8,128)}), f32[64,1,64,128]{3,2,1,0:T(8,128)S(1)}, u32[]{:S(2)}, u32[]{:S(2)}) async-start(f32[64,1,64,128]{3,2,1,0:T(8,128)} %copy.284), calls=%async_computation.19 | async-start | bytes 4194304 | tf_op jit(solution)/shard_map/all_to_all | solution.py:82
  427.6 49.7 %all-to-all-done.19 = f32[64,1,64,128]{3,2,1,0:T(8,128)S(1)} async-done(((f32[64,1,64,128]{3,2,1,0:T(8,128)}), f32[64,1,64,128]{3,2,1,0:T(8,128)S(1)}, u32[]{:S(2)}, u32[]{:S(2)}) %all-to-all-start.19) | async-done | bytes 2097184 | tf_op jit(solution)/shard_map/all_to_all | solution.py:82
  478.1 11.7 %custom-call.20 = f32[1,128,128]{2,1,0:T(8,128)S(1)} custom-call(f32[1,128,128]{2,1,0:T(8,128)S(1)} %fusion.54), custom_call_target="Cholesky" | custom-call | tf_op jit(solution)/shard_map/jit(cholesky)/cholesky | solution.py:290
  491.2 9.8 %custom-call.21 = f32[1,128,128]{1,2,0:T(8,128)S(1)} custom-call(f32[1,128,128]{2,1,0:T(8,128)S(1)} %select_select_fusion.1), custom_call_target="InvertDiagBlocksLowerTriangular" | custom-call | tf_op jit(solution)/shard_map/jit(_solve_triangular)/triangular_solve | solution.py:291
  515.5 7.6 all-to-all-done.25
  535.0 8.4 all_to_all.192
  549.8 26.5 %all-to-all-done.22 = f32[8,4,1,64,128]{4,3,1,2,0:T(8,128)S(1)} async-done(((f32[8,4,1,64,128]{4,3,1,2,0:T(8,128)}), f32[8,4,1,64,128]{4,3,1,2,0:T(8,128)S(1)}, u32[]{:S(2)}, u32[]{:S(2)}) %all-to-all-start.22) | async-done | bytes 1048608 | tf_op jit(solution)/shard_map/all_to_all | solution.py:28
  605.1 7.4 copy.330
  612.4 92.3 %while.54 = (s32[]{:T(128)}, f32[8,8,256]{2,1,0:T(8,128)S(1)}, f32[8,8]{1,0:T(8,128)S(1)}, f32[8,8,128,128]{2,3,1,0:T(8,128)}, f32[4,64,128]{2,1,0:T(8,128)S(1)}, /*index=5*/f32[8,8,128]{2,1,0:T(8,128)S(1)}, s32[]{:T(128)}) while((s32[]{:T(128)}, f32[8,8,256]{2,1,0:T(8,128)S(1)}, f32[8,8]{1,0:T(8,128)S(1)}, f32[8,8,128,128]{2,3,1,0:T(8,128)}, ...), condition=%wide.region_24.27_spmd, body=%wide.region_21.26_spmd.sunk | while | flops 403443200 | bytes 2803933 | solution.py:141
  614.7 7.4 copy.387
  626.2 7.4 copy.387
  637.7 7.4 copy.387
  649.3 7.4 copy.387
  660.8 7.4 copy.387
  672.3 7.4 copy.387
  683.9 7.4 copy.387
  695.4 7.4 copy.387
  718.0 31.7 %while.55 = (s32[]{:T(128)}, f32[8,8]{1,0:T(8,128)S(1)}, f32[8,8,128]{2,1,0:T(8,128)}, f32[8,8,128,128]{3,2,1,0:T(8,128)}, f32[8,8,256]{2,1,0:T(8,128)S(1)}, /*i...) while((s32[]{:T(128)}, f32[8,8]{1,0:T(8,128)S(1)}, ...), condition=%wide.region_29.32_spmd, body=%wide.region_27.31_spmd.sunk | while | flops 406849536 | bytes 1254601 | solution.py:167
  768.1 10.4 %all-to-all-start.34 = ((f32[64,1,64]{2,1,0:T(1,128)}), f32[64,1,64]{2,1,0:T(1,128)S(1)}, u32[]{:S(2)}, u32[]{:S(2)}) async-start(f32[64,1,64]{2,1,0:T(1,128)} %copy.319), calls=%async_computation.34 | async-start | bytes 65536 | tf_op jit(solution)/shard_map/all_to_all | solution.py:82
  787.1 9.4 %all-to-all-start.31 = ((f32[64,1,128]{2,1,0:T(1,128)}), f32[64,1,128]{2,1,0:T(1,128)S(1)}, u32[]{:S(2)}, u32[]{:S(2)}) async-start(f32[64,1,128]{2,1,0:T(1,128)} %bitcast.115), calls=%async_computation.31 | async-start | bytes 65536 | tf_op jit(solution)/shard_map/all_to_all | solution.py:82
  805.1 10.3 %all-to-all-start.33 = ((f32[64,1,64,128]{3,2,1,0:T(8,128)}), f32[64,1,64,128]{3,2,1,0:T(8,128)S(1)}, u32[]{:S(2)}, u32[]{:S(2)}) async-start(f32[64,1,64,128]{3,2,1,0:T(8,128)} %copy.313), calls=%async_computation.33 | async-start | bytes 4194304 | tf_op jit(solution)/shard_map/all_to_all | solution.py:82
  817.4 49.0 %all-to-all-done.33 = f32[64,1,64,128]{3,2,1,0:T(8,128)S(1)} async-done(((f32[64,1,64,128]{3,2,1,0:T(8,128)}), f32[64,1,64,128]{3,2,1,0:T(8,128)S(1)}, u32[]{:S(2)}, u32[]{:S(2)}) %all-to-all-start.33) | async-done | bytes 2097184 | tf_op jit(solution)/shard_map/all_to_all | solution.py:82
  867.2 11.7 %custom-call.22 = f32[1,128,128]{2,1,0:T(8,128)S(1)} custom-call(f32[1,128,128]{2,1,0:T(8,128)S(1)} %fusion.52), custom_call_target="Cholesky" | custom-call | tf_op jit(solution)/shard_map/jit(cholesky)/cholesky | solution.py:290
  880.3 9.8 %custom-call.23 = f32[1,128,128]{1,2,0:T(8,128)S(1)} custom-call(f32[1,128,128]{2,1,0:T(8,128)S(1)} %select_select_fusion), custom_call_target="InvertDiagBlocksLowerTriangular" | custom-call | tf_op jit(solution)/shard_map/jit(_solve_triangular)/triangular_solve | solution.py:291
  (503 shorter events, 403.8 us)
Async XLA Ops:
  0.6 83.4 %copy-start = (f32[1024,128]{1,0:T(8,128)S(1)}, f32[1024,128]{1,0:T(8,128)}, u32[]{:S(2)}) copy-start(f32[1024,128]{1,0:T(8,128)} %param.17) | copy-start | bytes 1572868
  1.9 9.1 %all-to-all-start = ((f32[4,1,1]{2,1,0:T(1,128)}), f32[4,1,1]{2,1,0:T(1,128)S(1)}, u32[]{:S(2)}, u32[]{:S(2)}) async-start(f32[4,1,1]{2,1,0:T(1,128)} %stack.72), calls=%async_computation | async-start | bytes 4096 | tf_op jit(solution)/shard_map/all_to_all | solution.py:28
  11.8 15.7 %all-to-all-start.1 = ((f32[8,4,1]{1,2,0:T(1,128)}), f32[8,4,1]{1,2,0:T(1,128)S(1)}, u32[]{:S(2)}, u32[]{:S(2)}) async-start(f32[8,4,1]{1,2,0:T(1,128)} %stack.73), calls=%async_computation.1 | async-start | bytes 8192 | tf_op jit(solution)/shard_map/all_to_all | solution.py:28
  28.0 8.4 all-to-all-start.6
  37.6 8.5 all-to-all-start.10
  43.0 39.4 %copy-start.7 = (s32[64]{0:T(128)S(1)}, s32[64]{0:T(128)}, u32[]{:S(2)}) copy-start(s32[64]{0:T(128)} %param.18) | copy-start | bytes 772
  46.1 11.0 %all-to-all-start.7 = ((f32[8,1,256]{2,1,0:T(1,128)}), f32[8,1,256]{2,1,0:T(1,128)S(1)}, u32[]{:S(2)}, u32[]{:S(2)}) async-start(f32[8,1,256]{2,1,0:T(1,128)} %reshape.971), calls=%async_computation.7 | async-start | bytes 16384 | tf_op jit(solution)/shard_map/all_to_all | solution.py:28
  49.5 33.5 %copy-start.5 = (s32[64,16]{0,1:T(8,128)S(1)}, s32[64,16]{0,1:T(8,128)}, u32[]{:S(2)}) copy-start(s32[64,16]{0,1:T(8,128)} %param.19) | copy-start | bytes 12292
  57.8 11.0 %all-to-all-start.11 = ((f32[8,4,1,128]{3,1,2,0:T(4,128)}), f32[8,4,1,128]{3,1,2,0:T(4,128)S(1)}, u32[]{:S(2)}, u32[]{:S(2)}) async-start(f32[8,4,1,128]{3,1,2,0:T(4,128)} %stack.82), calls=%async_computation.11 | async-start | bytes 32768 | tf_op jit(solution)/shard_map/all_to_all | solution.py:28
  78.1 25.1 %all-to-all-start.4 = ((f32[8,4,1,64,128]{4,3,1,2,0:T(8,128)}), f32[8,4,1,64,128]{4,3,1,2,0:T(8,128)}, u32[]{:S(2)}, u32[]{:S(2)}) async-start(f32[8,4,1,64,128]{4,3,1,2,0:T(8,128)} %stack.76), calls=%async_computation.4 | async-start | bytes 2097152 | tf_op jit(solution)/shard_map/all_to_all | solution.py:28
  103.3 6.4 all-to-all-start.2
  123.7 57.8 %all-to-all-start.9 = ((f32[64,1,64,128]{3,2,1,0:T(8,128)}), f32[64,1,64,128]{3,2,1,0:T(8,128)}, u32[]{:S(2)}, u32[]{:S(2)}) async-start(f32[64,1,64,128]{3,2,1,0:T(8,128)} %fusion.48), calls=%async_computation.9 | async-start | bytes 4194304 | tf_op jit(solution)/shard_map/all_to_all | solution.py:112
  276.7 9.8 %all-to-all-start.13 = ((f32[4,2,256]{2,1,0:T(2,128)}), f32[4,2,256]{2,1,0:T(2,128)S(1)}, u32[]{:S(2)}, u32[]{:S(2)}) async-start(f32[4,2,256]{2,1,0:T(2,128)} %broadcast_in_dim.201), calls=%async_computation.13 | async-start | bytes 16384 | tf_op jit(solution)/shard_map/all_to_all | solution.py:42
  344.5 16.4 %all-to-all-start.14 = ((f32[64,1,128]{2,1,0:T(1,128)}), f32[64,1,128]{2,1,0:T(1,128)S(1)}, u32[]{:S(2)}, u32[]{:S(2)}) async-start(f32[64,1,128]{2,1,0:T(1,128)} %bitcast.70), calls=%async_computation.14 | async-start | bytes 65536 | tf_op jit(solution)/shard_map/all_to_all | solution.py:82
  358.4 23.1 %copy-start.6 = (f32[1,128]{1,0:T(1,128)S(1)}, f32[1,128]{1,0:T(1,128)}, u32[]{:S(2)}) copy-start(f32[1,128]{1,0:T(1,128)} %param.20) | copy-start | bytes 1540
  361.5 14.6 %all-to-all-start.17 = ((f32[8,4,1]{1,2,0:T(1,128)}), f32[8,4,1]{1,2,0:T(1,128)S(1)}, u32[]{:S(2)}, u32[]{:S(2)}) async-start(f32[8,4,1]{1,2,0:T(1,128)} %stack.85), calls=%async_computation.17 | async-start | bytes 8192 | tf_op jit(solution)/shard_map/all_to_all | solution.py:28
  376.1 13.9 %all-to-all-start.20 = ((f32[64,1,64]{2,1,0:T(1,128)}), f32[64,1,64]{2,1,0:T(1,128)S(1)}, u32[]{:S(2)}, u32[]{:S(2)}) async-start(f32[64,1,64]{2,1,0:T(1,128)} %copy.290), calls=%async_computation.20 | async-start | bytes 65536 | tf_op jit(solution)/shard_map/all_to_all | solution.py:82
  390.6 12.4 %all-to-all-start.27 = ((f32[4,1,1,128]{3,2,1,0:T(1,128)}), f32[4,1,1,128]{3,2,1,0:T(1,128)S(1)}, u32[]{:S(2)}, u32[]{:S(2)}) async-start(f32[4,1,1,128]{3,2,1,0:T(1,128)} %stack.93), calls=%async_computation.27 | async-start | bytes 4096 | tf_op jit(solution)/shard_map/all_to_all | solution.py:28
  399.5 7.4 copy-start.3
  403.6 11.5 %all-to-all-start.28 = ((f32[8,4,1,128]{3,1,2,0:T(4,128)}), f32[8,4,1,128]{3,1,2,0:T(4,128)S(1)}, u32[]{:S(2)}, u32[]{:S(2)}) async-start(f32[8,4,1,128]{3,1,2,0:T(4,128)} %stack.94), calls=%async_computation.28 | async-start | bytes 32768 | tf_op jit(solution)/shard_map/all_to_all | solution.py:28
  415.1 62.3 %all-to-all-start.19 = ((f32[64,1,64,128]{3,2,1,0:T(8,128)}), f32[64,1,64,128]{3,2,1,0:T(8,128)S(1)}, u32[]{:S(2)}, u32[]{:S(2)}) async-start(f32[64,1,64,128]{3,2,1,0:T(8,128)} %copy.284), calls=%async_computation.19 | async-start | bytes 4194304 | tf_op jit(solution)/shard_map/all_to_all | solution.py:82
  502.8 8.6 all-to-all-start.24
  512.1 11.0 %all-to-all-start.25 = ((f32[8,1,256]{2,1,0:T(1,128)}), f32[8,1,256]{2,1,0:T(1,128)S(1)}, u32[]{:S(2)}, u32[]{:S(2)}) async-start(f32[8,1,256]{2,1,0:T(1,128)} %reshape.975), calls=%async_computation.25 | async-start | bytes 16384 | tf_op jit(solution)/shard_map/all_to_all | solution.py:28
  523.1 4.5 all-to-all-start.18
  544.5 31.8 %all-to-all-start.22 = ((f32[8,4,1,64,128]{4,3,1,2,0:T(8,128)}), f32[8,4,1,64,128]{4,3,1,2,0:T(8,128)S(1)}, u32[]{:S(2)}, u32[]{:S(2)}) async-start(f32[8,4,1,64,128]{4,3,1,2,0:T(8,128)} %stack.88), calls=%async_computation.22 | async-start | bytes 2097152 | tf_op jit(solution)/shard_map/all_to_all | solution.py:28
  595.9 3.4 copy-start.2
  705.4 8.7 all-to-all-start.30
  750.4 17.7 %all-to-all-start.32 = ((f32[64,1,1]{2,1,0:T(1,128)}), f32[64,1,1]{2,1,0:T(1,128)S(1)}, u32[]{:S(2)}, u32[]{:S(2)}) async-start(f32[64,1,1]{2,1,0:T(1,128)} %all_to_all.149), calls=%async_computation.32 | async-start | bytes 65536 | tf_op jit(solution)/shard_map/all_to_all | solution.py:82
  768.1 19.0 %all-to-all-start.34 = ((f32[64,1,64]{2,1,0:T(1,128)}), f32[64,1,64]{2,1,0:T(1,128)S(1)}, u32[]{:S(2)}, u32[]{:S(2)}) async-start(f32[64,1,64]{2,1,0:T(1,128)} %copy.319), calls=%async_computation.34 | async-start | bytes 65536 | tf_op jit(solution)/shard_map/all_to_all | solution.py:82
  782.7 13.8 %copy-start.4 = (f32[64,64,64]{0,2,1:T(8,128)S(1)}, f32[64,64,64]{0,2,1:T(8,128)}, u32[]{:S(2)}) copy-start(f32[64,64,64]{0,2,1:T(8,128)} %select_add_fusion) | copy-start | bytes 3145732
  787.1 18.0 %all-to-all-start.31 = ((f32[64,1,128]{2,1,0:T(1,128)}), f32[64,1,128]{2,1,0:T(1,128)S(1)}, u32[]{:S(2)}, u32[]{:S(2)}) async-start(f32[64,1,128]{2,1,0:T(1,128)} %bitcast.115), calls=%async_computation.31 | async-start | bytes 65536 | tf_op jit(solution)/shard_map/all_to_all | solution.py:82
  805.1 61.4 %all-to-all-start.33 = ((f32[64,1,64,128]{3,2,1,0:T(8,128)}), f32[64,1,64,128]{3,2,1,0:T(8,128)S(1)}, u32[]{:S(2)}, u32[]{:S(2)}) async-start(f32[64,1,64,128]{3,2,1,0:T(8,128)} %copy.313), calls=%async_computation.33 | async-start | bytes 4194304 | tf_op jit(solution)/shard_map/all_to_all | solution.py:82
  815.3 75.8 %copy-start.1 = (f32[1024,128]{1,0:T(8,128)S(1)}, f32[1024,128]{1,0:T(8,128)}, u32[]{:S(2)}) copy-start(f32[1024,128]{1,0:T(8,128)} %param.17) | copy-start | bytes 1572868
